TPU v7x, 128 devices: a whole 4x4x4 slice. The times are simulated.
128 devices in a mesh: blk: 8 (over z, y_hi), rows: 16 (over x, y_lo, core).
Axes of the slice: x: 4, y: 4 (y_hi: 2, y_lo: 2; y = y_hi * 2 + y_lo), z: 4, core: 2. Of those that a mesh axis runs over, the one named last changes fastest.
Arguments:
- embeddings: bfloat16 [65536, 768], P(('blk', 'rows')), as said below
- centroids: bfloat16 [8192, 768], P('blk'), as said below
- log_mix: float32 [8192], P('blk'), may hold values from -1.5 to 3.7
Outputs:
- new_centroids: float32 [8192, 768], P('blk')
- new_weights: float32 [8192], P('blk')
Inputs may be any that keep to these rules, and one draw needn't show every extreme that they name: `embeddings`: real vectors of no fixed length. `centroids`: real vectors of no fixed length.
All inputs are finite; a program needn't handle non-finite values.
Results may differ from a plain program's by a relative error of at most 0.0024.
Values may be sent and summed in bfloat16 or wider, within the bound.
A program may use at most 64 MiB of HBM per device.

v0:
```python
import math
import jax
import jax.numpy as jnp
from jax import lax
from jax.sharding import PartitionSpec as P

K = 8192
concentration = 32.0


def sent_to_all(x, axis):
    count = lax.axis_size(axis)
    return lax.all_to_all(jnp.broadcast_to(x[None], (count, *x.shape)), axis, 0, 0, tiled=True)


def of_everyone(x, axis):
    everything = sent_to_all(x, axis)
    return jnp.sum(everything, axis=0)


def split_up(x, dim, count):
    lengths = x.shape
    pieces = x.reshape(*lengths[:dim], count, lengths[dim] // count, *lengths[dim + 1 :])
    return jnp.moveaxis(pieces, dim, 0)


def summed_on_arrival(x, axis, dim):
    pieces = split_up(x, dim, lax.axis_size(axis))
    arrived = lax.all_to_all(pieces, axis, split_axis=0, concat_axis=0, tiled=True)
    return arrived.sum(axis=0)


def side_by_side(arrays, axis, dim, along):
    widths = [math.prod(a.shape[along:]) for a in arrays]
    both = jnp.concatenate(
        [a.reshape(*a.shape[:along], w) for a, w in zip(arrays, widths)], axis=along
    )
    filled = summed_on_arrival(both, axis, dim)
    pieces = jnp.split(filled, [sum(widths[:k]) for k in range(1, len(widths))], axis=along)
    return tuple(
        (b.reshape(*filled.shape[:along], *a.shape[along:]) for a, b in zip(arrays, pieces))
    )


def side_by_side_2(arrays, axis, dim, along):
    widths = [math.prod(a.shape[along:]) for a in arrays]
    both = jnp.concatenate(
        [a.reshape(*a.shape[:along], w) for a, w in zip(arrays, widths)], axis=along
    )
    filled = lax.all_gather(both, axis, axis=dim, tiled=True)
    pieces = jnp.split(filled, [sum(widths[:k]) for k in range(1, len(widths))], axis=along)
    return tuple(
        (b.reshape(*filled.shape[:along], *a.shape[along:]) for a, b in zip(arrays, pieces))
    )


def to_unit(values):
    values = values.astype(jnp.float32)
    return (values * lax.rsqrt(jnp.sum(values * values, axis=-1, keepdims=True) + 1e-06)).astype(
        jnp.bfloat16
    )


def finish(weighted, masses, factor):
    new_centroids = weighted * lax.rsqrt(
        jnp.sum(weighted * weighted, axis=1, keepdims=True) + 1e-06
    )
    return (new_centroids, masses * factor)


def local(embeddings, centroids, log_mix):
    centroid_units = to_unit(centroids)
    row_units = to_unit(embeddings)
    gathered = lax.all_gather(row_units, "blk", axis=0, tiled=True)
    row_total = gathered.shape[0]
    block_rows = math.gcd(row_total, 512)
    grouped = gathered.reshape(row_total // block_rows, block_rows, gathered.shape[1])

    def exponents(row_block):
        cosines = lax.dot_general(
            row_block, centroid_units, (((1,), (1,)), ((), ())), preferred_element_type=jnp.float32
        )
        return jnp.exp(log_mix[None, :] + concentration * (cosines - 1.0))

    def add_block(carried, resp, row_block):
        weighted = carried[0] + lax.dot_general(
            resp, row_block, (((0,), (0,)), ((), ())), preferred_element_type=jnp.float32
        )
        masses = carried[1] + jnp.sum(resp.astype(jnp.float32), axis=0)
        return (weighted, masses)

    local_centroids = centroids.shape[0]
    start_state = (
        jnp.zeros((local_centroids, centroids.shape[1]), jnp.float32),
        jnp.zeros((local_centroids,), jnp.float32),
    )
    partial_sums = lax.map(lambda row_block: jnp.sum(exponents(row_block), axis=1), grouped)
    totals = of_everyone(partial_sums, "blk")

    def accumulate(carried, element):
        row_block, block_totals = element
        resp = (exponents(row_block) / block_totals[:, None]).astype(jnp.bfloat16)
        return (add_block(carried, resp, row_block), None)

    (weighted, masses), _ = lax.scan(accumulate, start_state, (grouped, totals))
    factor = K / (row_total * lax.axis_size("rows"))
    share, share_masses = side_by_side((weighted, masses), "rows", 0, 1)
    new_share, weight_share = finish(share, share_masses, factor)
    return side_by_side_2((new_share, weight_share), "rows", 0, 1)


def solution(mesh):
    return jax.shard_map(
        local,
        mesh=mesh,
        in_specs=(P(("blk", "rows"), None), P("blk", None), P("blk")),
        out_specs=(P("blk", None), P("blk")),
        check_vma=False,
    )
```

profile of v0, /device:TPU:1, one launch (start us, length us, event | category | flops | bytes accessed | tf_op | source)
XLA Modules:
  0.0 282.0 jit_solution(1519887824641105736)
XLA Ops:
  11.7 90.6 %all-gather.3.cloned.1.call-done = bf16[4096,768]{1,0:T(8,128)(2,1)} async-done(((bf16[512,768]{1,0:T(8,128)(2,1)}), bf16[4096,768]{1,0:T(8,128)(2,1)}) %all-gather.3.cloned.1.call-update) | async-done | bytes 6291472 | tf_op jit(solution)/shard_map/all_gather | solution.py:74
  102.3 19.3 %while.27 = (s32[]{:T(128)}, f32[8,512]{1,0:T(8,128)S(1)}, f32[1024]{0:T(1024)S(1)}, bf16[8,512,768]{2,1,0:T(8,128)(2,1)}, bf16[1024,768]{1,0:T(8,128)(2,1)S(1)}, /*index=5*/s32[]{:T(128)}, s32[]{:T(128)}) while((s32[]{:T(128)}, f32[8,512]{1,0:T(8,128)S(1)}, f32[1024]{0:T(1024)S(1)}, bf16[8,512,768]{2,1,0:T(8,128)(2,1)}, ...), condition=%wide.region_4.5_spmd, body=%wide.region_2.4_spmd.sunk | while | flops 807403008 | bytes 2369629 | solution.py:97
  122.3 3.4 %all-to-all-start = ((f32[8,8,512]{2,1,0:T(8,128)}), f32[8,8,512]{2,1,0:T(8,128)S(1)}, u32[]{:S(2)}, u32[]{:S(2)}) async-start(f32[8,8,512]{2,1,0:T(8,128)} %broadcast_in_dim.31), calls=%async_computation | async-start | bytes 262144 | tf_op jit(solution)/shard_map/all_to_all | solution.py:13
  125.8 6.9 %all-to-all-done = f32[8,8,512]{2,1,0:T(8,128)S(1)} async-done(((f32[8,8,512]{2,1,0:T(8,128)}), f32[8,8,512]{2,1,0:T(8,128)S(1)}, u32[]{:S(2)}, u32[]{:S(2)}) %all-to-all-start) | async-done | bytes 131104 | tf_op jit(solution)/shard_map/all_to_all | solution.py:13
  132.7 47.6 %while.28 = (s32[]{:T(128)}, f32[1024,768]{1,0:T(8,128)S(1)}, f32[1024]{0:T(1024)S(1)}, f32[1024]{0:T(1024)S(1)}, bf16[8,512,768]{2,1,0:T(8,128)(2,1)}, /*index=...) while((s32[]{:T(128)}, f32[1024,768]{1,0:T(8,128)S(1)}, ...), condition=%wide.region_8.9_spmd.clone, body=%wide.region_6.8_spmd.clone.sunk | while | flops 1615856640 | bytes 11561084 | solution.py:105
  132.7 2.9 %convert_reduce_fusion.2 = (f32[1024]{0:T(1024)S(1)}, bf16[512,1024]{1,0:T(8,128)(2,1)S(1)}) fusion(f32[512]{0:T(512)S(1)} %bitcast.36, bf16[1024,768]{1,0:T(8,128)(2,1)} %get-tuple-element.332, bf16[8,512,768]{2,1,0:T(8,128)(2,1)} %get-tuple-element.331, s32[]{:T(128)S(6)} %copy.17, f32[1024]{0:T(1024)S(1)} %get-tuple-element.330), kind=kOutput, calls=%fused_computation.5.clone.1 | convolution fusion | flops 808975360 | bytes 3418116 | tf_op jit(solution)/shard_map/while/body/eval_jaxpr/dot_general | solution.py:80
  135.6 3.0 %select_add_fusion.4 = f32[1024,768]{1,0:T(8,128)S(1)} fusion(f32[1024,768]{1,0:T(8,128)S(1)} %get-tuple-element.319, bf16[512,1024]{1,0:T(8,128)(2,1)S(1)} %get-tuple-element.286, pred[]{:T(512)S(6)} %compare.3, bf16[8,512,768]{2,1,0:T(8,128)(2,1)} %get-tuple-element.331, s32[]{:T(128)S(6)} %copy.17), kind=kOutput, calls=%fused_computation.4.clone.1 | convolution fusion | flops 806879232 | bytes 8126469 | tf_op jit(solution)/shard_map/while/body/eval_jaxpr/dot_general | solution.py:86
  138.7 2.9 %convert_reduce_fusion.2 = (f32[1024]{0:T(1024)S(1)}, bf16[512,1024]{1,0:T(8,128)(2,1)S(1)}) fusion(f32[512]{0:T(512)S(1)} %bitcast.36, bf16[1024,768]{1,0:T(8,128)(2,1)} %get-tuple-element.332, bf16[8,512,768]{2,1,0:T(8,128)(2,1)} %get-tuple-element.331, s32[]{:T(128)S(6)} %copy.17, f32[1024]{0:T(1024)S(1)} %get-tuple-element.330), kind=kOutput, calls=%fused_computation.5.clone.1 | convolution fusion | flops 808975360 | bytes 3418116 | tf_op jit(solution)/shard_map/while/body/eval_jaxpr/dot_general | solution.py:80
  141.6 3.0 %select_add_fusion.4 = f32[1024,768]{1,0:T(8,128)S(1)} fusion(f32[1024,768]{1,0:T(8,128)S(1)} %get-tuple-element.319, bf16[512,1024]{1,0:T(8,128)(2,1)S(1)} %get-tuple-element.286, pred[]{:T(512)S(6)} %compare.3, bf16[8,512,768]{2,1,0:T(8,128)(2,1)} %get-tuple-element.331, s32[]{:T(128)S(6)} %copy.17), kind=kOutput, calls=%fused_computation.4.clone.1 | convolution fusion | flops 806879232 | bytes 8126469 | tf_op jit(solution)/shard_map/while/body/eval_jaxpr/dot_general | solution.py:86
  144.6 2.9 %convert_reduce_fusion.2 = (f32[1024]{0:T(1024)S(1)}, bf16[512,1024]{1,0:T(8,128)(2,1)S(1)}) fusion(f32[512]{0:T(512)S(1)} %bitcast.36, bf16[1024,768]{1,0:T(8,128)(2,1)} %get-tuple-element.332, bf16[8,512,768]{2,1,0:T(8,128)(2,1)} %get-tuple-element.331, s32[]{:T(128)S(6)} %copy.17, f32[1024]{0:T(1024)S(1)} %get-tuple-element.330), kind=kOutput, calls=%fused_computation.5.clone.1 | convolution fusion | flops 808975360 | bytes 3418116 | tf_op jit(solution)/shard_map/while/body/eval_jaxpr/dot_general | solution.py:80
  147.5 3.0 %select_add_fusion.4 = f32[1024,768]{1,0:T(8,128)S(1)} fusion(f32[1024,768]{1,0:T(8,128)S(1)} %get-tuple-element.319, bf16[512,1024]{1,0:T(8,128)(2,1)S(1)} %get-tuple-element.286, pred[]{:T(512)S(6)} %compare.3, bf16[8,512,768]{2,1,0:T(8,128)(2,1)} %get-tuple-element.331, s32[]{:T(128)S(6)} %copy.17), kind=kOutput, calls=%fused_computation.4.clone.1 | convolution fusion | flops 806879232 | bytes 8126469 | tf_op jit(solution)/shard_map/while/body/eval_jaxpr/dot_general | solution.py:86
  150.6 2.9 %convert_reduce_fusion.2 = (f32[1024]{0:T(1024)S(1)}, bf16[512,1024]{1,0:T(8,128)(2,1)S(1)}) fusion(f32[512]{0:T(512)S(1)} %bitcast.36, bf16[1024,768]{1,0:T(8,128)(2,1)} %get-tuple-element.332, bf16[8,512,768]{2,1,0:T(8,128)(2,1)} %get-tuple-element.331, s32[]{:T(128)S(6)} %copy.17, f32[1024]{0:T(1024)S(1)} %get-tuple-element.330), kind=kOutput, calls=%fused_computation.5.clone.1 | convolution fusion | flops 808975360 | bytes 3418116 | tf_op jit(solution)/shard_map/while/body/eval_jaxpr/dot_general | solution.py:80
  153.5 3.0 %select_add_fusion.4 = f32[1024,768]{1,0:T(8,128)S(1)} fusion(f32[1024,768]{1,0:T(8,128)S(1)} %get-tuple-element.319, bf16[512,1024]{1,0:T(8,128)(2,1)S(1)} %get-tuple-element.286, pred[]{:T(512)S(6)} %compare.3, bf16[8,512,768]{2,1,0:T(8,128)(2,1)} %get-tuple-element.331, s32[]{:T(128)S(6)} %copy.17), kind=kOutput, calls=%fused_computation.4.clone.1 | convolution fusion | flops 806879232 | bytes 8126469 | tf_op jit(solution)/shard_map/while/body/eval_jaxpr/dot_general | solution.py:86
  156.5 2.9 %convert_reduce_fusion.2 = (f32[1024]{0:T(1024)S(1)}, bf16[512,1024]{1,0:T(8,128)(2,1)S(1)}) fusion(f32[512]{0:T(512)S(1)} %bitcast.36, bf16[1024,768]{1,0:T(8,128)(2,1)} %get-tuple-element.332, bf16[8,512,768]{2,1,0:T(8,128)(2,1)} %get-tuple-element.331, s32[]{:T(128)S(6)} %copy.17, f32[1024]{0:T(1024)S(1)} %get-tuple-element.330), kind=kOutput, calls=%fused_computation.5.clone.1 | convolution fusion | flops 808975360 | bytes 3418116 | tf_op jit(solution)/shard_map/while/body/eval_jaxpr/dot_general | solution.py:80
  159.4 3.0 %select_add_fusion.4 = f32[1024,768]{1,0:T(8,128)S(1)} fusion(f32[1024,768]{1,0:T(8,128)S(1)} %get-tuple-element.319, bf16[512,1024]{1,0:T(8,128)(2,1)S(1)} %get-tuple-element.286, pred[]{:T(512)S(6)} %compare.3, bf16[8,512,768]{2,1,0:T(8,128)(2,1)} %get-tuple-element.331, s32[]{:T(128)S(6)} %copy.17), kind=kOutput, calls=%fused_computation.4.clone.1 | convolution fusion | flops 806879232 | bytes 8126469 | tf_op jit(solution)/shard_map/while/body/eval_jaxpr/dot_general | solution.py:86
  162.5 2.9 %convert_reduce_fusion.2 = (f32[1024]{0:T(1024)S(1)}, bf16[512,1024]{1,0:T(8,128)(2,1)S(1)}) fusion(f32[512]{0:T(512)S(1)} %bitcast.36, bf16[1024,768]{1,0:T(8,128)(2,1)} %get-tuple-element.332, bf16[8,512,768]{2,1,0:T(8,128)(2,1)} %get-tuple-element.331, s32[]{:T(128)S(6)} %copy.17, f32[1024]{0:T(1024)S(1)} %get-tuple-element.330), kind=kOutput, calls=%fused_computation.5.clone.1 | convolution fusion | flops 808975360 | bytes 3418116 | tf_op jit(solution)/shard_map/while/body/eval_jaxpr/dot_general | solution.py:80
  165.4 3.0 %select_add_fusion.4 = f32[1024,768]{1,0:T(8,128)S(1)} fusion(f32[1024,768]{1,0:T(8,128)S(1)} %get-tuple-element.319, bf16[512,1024]{1,0:T(8,128)(2,1)S(1)} %get-tuple-element.286, pred[]{:T(512)S(6)} %compare.3, bf16[8,512,768]{2,1,0:T(8,128)(2,1)} %get-tuple-element.331, s32[]{:T(128)S(6)} %copy.17), kind=kOutput, calls=%fused_computation.4.clone.1 | convolution fusion | flops 806879232 | bytes 8126469 | tf_op jit(solution)/shard_map/while/body/eval_jaxpr/dot_general | solution.py:86
  168.4 2.9 %convert_reduce_fusion.2 = (f32[1024]{0:T(1024)S(1)}, bf16[512,1024]{1,0:T(8,128)(2,1)S(1)}) fusion(f32[512]{0:T(512)S(1)} %bitcast.36, bf16[1024,768]{1,0:T(8,128)(2,1)} %get-tuple-element.332, bf16[8,512,768]{2,1,0:T(8,128)(2,1)} %get-tuple-element.331, s32[]{:T(128)S(6)} %copy.17, f32[1024]{0:T(1024)S(1)} %get-tuple-element.330), kind=kOutput, calls=%fused_computation.5.clone.1 | convolution fusion | flops 808975360 | bytes 3418116 | tf_op jit(solution)/shard_map/while/body/eval_jaxpr/dot_general | solution.py:80
  171.4 3.0 %select_add_fusion.4 = f32[1024,768]{1,0:T(8,128)S(1)} fusion(f32[1024,768]{1,0:T(8,128)S(1)} %get-tuple-element.319, bf16[512,1024]{1,0:T(8,128)(2,1)S(1)} %get-tuple-element.286, pred[]{:T(512)S(6)} %compare.3, bf16[8,512,768]{2,1,0:T(8,128)(2,1)} %get-tuple-element.331, s32[]{:T(128)S(6)} %copy.17), kind=kOutput, calls=%fused_computation.4.clone.1 | convolution fusion | flops 806879232 | bytes 8126469 | tf_op jit(solution)/shard_map/while/body/eval_jaxpr/dot_general | solution.py:86
  174.4 2.9 %convert_reduce_fusion.2 = (f32[1024]{0:T(1024)S(1)}, bf16[512,1024]{1,0:T(8,128)(2,1)S(1)}) fusion(f32[512]{0:T(512)S(1)} %bitcast.36, bf16[1024,768]{1,0:T(8,128)(2,1)} %get-tuple-element.332, bf16[8,512,768]{2,1,0:T(8,128)(2,1)} %get-tuple-element.331, s32[]{:T(128)S(6)} %copy.17, f32[1024]{0:T(1024)S(1)} %get-tuple-element.330), kind=kOutput, calls=%fused_computation.5.clone.1 | convolution fusion | flops 808975360 | bytes 3418116 | tf_op jit(solution)/shard_map/while/body/eval_jaxpr/dot_general | solution.py:80
  177.3 3.0 %select_add_fusion.4 = f32[1024,768]{1,0:T(8,128)S(1)} fusion(f32[1024,768]{1,0:T(8,128)S(1)} %get-tuple-element.319, bf16[512,1024]{1,0:T(8,128)(2,1)S(1)} %get-tuple-element.286, pred[]{:T(512)S(6)} %compare.3, bf16[8,512,768]{2,1,0:T(8,128)(2,1)} %get-tuple-element.331, s32[]{:T(128)S(6)} %copy.17), kind=kOutput, calls=%fused_computation.4.clone.1 | convolution fusion | flops 806879232 | bytes 8126469 | tf_op jit(solution)/shard_map/while/body/eval_jaxpr/dot_general | solution.py:86
  182.8 50.4 %all_to_all.10 = f32[16,64,769]{2,1,0:T(8,128)} all-to-all(f32[16,64,769]{2,1,0:T(8,128)S(1)} %pad_maximum_fusion), channel_id=1, replica_groups=mesh['blk'=8,'rows'=16] {'rows'}, dimensions={0} | all-to-all | bytes 6299648 | tf_op jit(solution)/shard_map/all_to_all | solution.py:29
  236.5 33.2 %all-gather.5.cloned.1.call-done = f32[1024,769]{1,0:T(8,128)} async-done(((f32[64,769]{1,0:T(8,128)}), f32[1024,769]{1,0:T(8,128)}) %all-gather.5.cloned.1.call-update) | async-done | bytes 3149840 | tf_op jit(solution)/shard_map/all_gather | solution.py:50
  271.5 3.8 %split.18 = f32[1024,768]{1,0:T(8,128)} slice(f32[1024,769]{1,0:T(8,128)} %all-gather.5.cloned.1.call-done), slice={[0:1024], [0:768]} | slice | bytes 6291456 | tf_op jit(solution)/shard_map/split | solution.py:51
  (62 shorter events, 31.9 us)
Async XLA Ops:
  7.2 3.8 %copy-start = (bf16[1024,768]{1,0:T(8,128)(2,1)S(1)}, bf16[1024,768]{1,0:T(8,128)(2,1)}, u32[]{:S(2)}) copy-start(bf16[1024,768]{1,0:T(8,128)(2,1)} %param.8) | copy-start | bytes 4718596
  7.2 95.2 %all-gather.3.cloned.1.call-start = ((), (), s32[]{:S(2)}) async-start(), calls=%async_computation.2 | async-start | bytes 7077888 | tf_op jit(solution)/shard_map/all_gather | solution.py:74
  11.0 91.4 %copy-start.2 = (f32[1024]{0:T(1024)S(1)}, f32[1024]{0:T(1024)}, u32[]{:S(2)}) copy-start(f32[1024]{0:T(1024)} %param.9) | copy-start | bytes 12292
  121.6 4.2 %copy-start.1 = (bf16[1024,768]{1,0:T(8,128)(2,1)}, bf16[1024,768]{1,0:T(8,128)(2,1)S(1)}, u32[]{:S(2)}) copy-start(bf16[1024,768]{1,0:T(8,128)(2,1)S(1)} %get-tuple-element.343) | copy-start | bytes 4718596
  122.3 10.4 %all-to-all-start = ((f32[8,8,512]{2,1,0:T(8,128)}), f32[8,8,512]{2,1,0:T(8,128)S(1)}, u32[]{:S(2)}, u32[]{:S(2)}) async-start(f32[8,8,512]{2,1,0:T(8,128)} %broadcast_in_dim.31), calls=%async_computation | async-start | bytes 262144 | tf_op jit(solution)/shard_map/all_to_all | solution.py:13
  125.7 143.9 %all-gather.5.cloned.1.call-start = ((), (), s32[]{:S(2)}) async-start(), calls=%async_computation.3 | async-start | bytes 3899392 | tf_op jit(solution)/shard_map/all_gather | solution.py:50
Sparse Core Ops, SparseCore 0:
  11.1 91.2 all-gather.2
  236.6 32.9 all-gather.4
where the time goes:
time: 283 us; the launch traced here: 282 us
  waiting for transfers between devices  131 us (46%)
  matrix products  65.8 us (23%)
  blocking collectives  50.4 us (18%)
  between operations  14.2 us (5%)
  other arithmetic  8.97 us (3%)
  local copies, waits for them, and re-layouts  7.99 us (3%)
  starting transfers between devices  3.45 us (1%)
    all_gather x1, waiting for transfers between devices, local(): gathered = lax.all_gather(row_units, 'blk', axis=0, tiled=True)  90.6 us
    all_to_all x1, blocking collectives, summed_on_arrival(): lax.all_to_all(pieces, axis, split_axis=0, concat_axis=0, tiled=True)  50.4 us
    dot_general x16, matrix products, exponents(): lax.dot_general(row_block, centroid_units, (((1,), (1,)), ((), ())), pref...  41.7 us
    all_gather x1, waiting for transfers between devices, side_by_side_2(): filled = lax.all_gather(both, axis, axis=dim, tiled=True)  33.2 us
    dot_general x8, matrix products, add_block(): lax.dot_general(resp, row_block, (((0,), (0,)), ((), ())), preferred_elem...  24 us
    all_to_all x1, waiting for transfers between devices, sent_to_all(): lax.all_to_all(jnp.broadcast_to(x[None], (count, *x.shape)), axis, 0, 0,...  6.9 us
  transfers between devices with their start and end apart: 3, of which 3 were waited for; matrix products, arithmetic and copies ran while one was open for 0% of the time, Pallas kernels for 0%

commit v1 on v0

--- a/solution.py
+++ b/solution.py
@@ -71,7 +71,9 @@
 def local(embeddings, centroids, log_mix):
     centroid_units = to_unit(centroids)
     row_units = to_unit(embeddings)
-    gathered = lax.all_gather(row_units, "blk", axis=0, tiled=True)
+    gathered = jnp.concatenate(
+        lax.all_to_all(jnp.stack([row_units] * lax.axis_size("blk")), "blk", 0, 0), axis=0
+    )
     row_total = gathered.shape[0]
     block_rows = math.gcd(row_total, 512)
     grouped = gathered.reshape(row_total // block_rows, block_rows, gathered.shape[1])

time: 283 us -> 286 us (1.011)
  waiting for transfers between devices: 131 us -> 112 us
  matrix products: 65.8 us -> 76.1 us
  starting transfers between devices: 3.45 us -> 12.4 us
  local copies, waits for them, and re-layouts: 7.99 us -> 11 us
    all_gather x1 -> x0, waiting for transfers between devices: 90.6 us -> none  [local(): gathered = lax.all_gather(row_units, 'blk', axis=0, tiled=True)]
    all_to_all x0 -> x1, waiting for transfers between devices: none -> 71.9 us  [local(): lax.all_to_all(jnp.stack([row_units] * lax.axis_size('blk')), 'blk', 0, 0)]
    all_to_all x0 -> x1, starting transfers between devices: none -> 8.61 us  [local(): lax.all_to_all(jnp.stack([row_units] * lax.axis_size('blk')), 'blk', 0, 0)]
    dot_general x16, matrix products: 41.7 us -> 49.8 us  [exponents(): lax.dot_general(row_block, centroid_units, (((1,), (1,)), ((), ())), pref...]
    another operation x0 -> x1, local copies, waits for them, and re-layouts: none -> 3.06 us  [local(): jnp.stack([row_units] * lax.axis_size('blk'))]
where the time goes in v1:
time: 286 us; the launch traced here: 284 us
  waiting for transfers between devices  112 us (39%)
  matrix products  76.1 us (27%)
  blocking collectives  50.3 us (18%)
  between operations  14.1 us (5%)
  starting transfers between devices  12.4 us (4%)
  local copies, waits for them, and re-layouts  11 us (4%)
  other arithmetic  7.98 us (3%)
    all_to_all x1, waiting for transfers between devices, local(): lax.all_to_all(jnp.stack([row_units] * lax.axis_size('blk')), 'blk', 0, 0)  71.9 us
    all_to_all x1, blocking collectives, summed_on_arrival(): lax.all_to_all(pieces, axis, split_axis=0, concat_axis=0, tiled=True)  50.3 us
    dot_general x16, matrix products, exponents(): lax.dot_general(row_block, centroid_units, (((1,), (1,)), ((), ())), pref...  49.8 us
    all_gather x1, waiting for transfers between devices, side_by_side_2(): filled = lax.all_gather(both, axis, axis=dim, tiled=True)  33.1 us
    dot_general x8, matrix products, add_block(): lax.dot_general(resp, row_block, (((0,), (0,)), ((), ())), preferred_elem...  26.4 us
    all_to_all x1, starting transfers between devices, local(): lax.all_to_all(jnp.stack([row_units] * lax.axis_size('blk')), 'blk', 0, 0)  8.61 us
    all_to_all x1, waiting for transfers between devices, sent_to_all(): lax.all_to_all(jnp.broadcast_to(x[None], (count, *x.shape)), axis, 0, 0,...  6.98 us
  transfers between devices with their start and end apart: 3, of which 3 were waited for; matrix products, arithmetic and copies ran while one was open for 0% of the time, Pallas kernels for 0%

profile of v1, /device:TPU:1, one launch (start us, length us, event | category | flops | bytes accessed | tf_op | source)
XLA Modules:
  0.0 284.5 jit_solution(6106601125382068198)
XLA Ops:
  12.9 8.6 %all-to-all-start = ((bf16[8,512,768]{2,1,0:T(8,128)(2,1)}), bf16[8,512,768]{2,1,0:T(8,128)(2,1)}, u32[]{:S(2)}, u32[]{:S(2)}) async-start(bf16[8,512,768]{2,1,0:T(8,128)(2,1)} %stack.2), calls=%async_computation | async-start | bytes 12582912 | tf_op jit(solution)/shard_map/all_to_all | solution.py:75
  22.3 71.9 %all-to-all-done = bf16[8,512,768]{2,1,0:T(8,128)(2,1)} async-done(((bf16[8,512,768]{2,1,0:T(8,128)(2,1)}), bf16[8,512,768]{2,1,0:T(8,128)(2,1)}, u32[]{:S(2)}, u32[]{:S(2)}) %all-to-all-start) | async-done | bytes 6291488 | tf_op jit(solution)/shard_map/all_to_all | solution.py:75
  94.2 19.2 %while.27 = (s32[]{:T(128)}, f32[8,512]{1,0:T(8,128)S(1)}, f32[1024]{0:T(1024)S(1)}, bf16[8,512,768]{2,1,0:T(8,128)(2,1)}, bf16[1024,768]{1,0:T(8,128)(2,1)S(1)}, /*index=5*/s32[]{:T(128)}, s32[]{:T(128)}) while((s32[]{:T(128)}, f32[8,512]{1,0:T(8,128)S(1)}, f32[1024]{0:T(1024)S(1)}, bf16[8,512,768]{2,1,0:T(8,128)(2,1)}, ...), condition=%wide.region_4.5_spmd, body=%wide.region_2.4_spmd.sunk | while | flops 807403008 | bytes 2370129 | solution.py:99
  114.2 3.8 %all-to-all-start.1 = ((f32[8,8,512]{2,1,0:T(8,128)}), f32[8,8,512]{2,1,0:T(8,128)S(1)}, u32[]{:S(2)}, u32[]{:S(2)}) async-start(f32[8,8,512]{2,1,0:T(8,128)} %broadcast_in_dim.31), calls=%async_computation.1 | async-start | bytes 262144 | tf_op jit(solution)/shard_map/all_to_all | solution.py:13
  118.0 7.0 %all-to-all-done.1 = f32[8,8,512]{2,1,0:T(8,128)S(1)} async-done(((f32[8,8,512]{2,1,0:T(8,128)}), f32[8,8,512]{2,1,0:T(8,128)S(1)}, u32[]{:S(2)}, u32[]{:S(2)}) %all-to-all-start.1) | async-done | bytes 131104 | tf_op jit(solution)/shard_map/all_to_all | solution.py:13
  125.0 57.9 %while.28 = (s32[]{:T(128)}, f32[1024,768]{1,0:T(8,128)S(1)}, f32[1024]{0:T(1024)S(1)}, f32[1024]{0:T(1024)S(1)}, bf16[8,512,768]{2,1,0:T(8,128)(2,1)}, /*index=...) while((s32[]{:T(128)}, f32[1024,768]{1,0:T(8,128)S(1)}, ...), condition=%wide.region_8.9_spmd.clone, body=%wide.region_6.8_spmd.clone.sunk | while | flops 1615856640 | bytes 11562092 | solution.py:107
  125.0 3.9 %convert_reduce_fusion.2 = (f32[1024]{0:T(1024)S(1)}, bf16[512,1024]{1,0:T(8,128)(2,1)}) fusion(f32[512]{0:T(512)S(1)} %bitcast.34, bf16[1024,768]{1,0:T(8,128)(2,1)} %get-tuple-element.332, bf16[8,512,768]{2,1,0:T(8,128)(2,1)} %get-tuple-element.331, s32[]{:T(128)} %get-tuple-element.318, f32[1024]{0:T(1024)S(1)} %get-tuple-element.330), kind=kOutput, calls=%fused_computation.5.clone.1 | convolution fusion | flops 808975360 | bytes 3418624 | tf_op jit(solution)/shard_map/while/body/eval_jaxpr/dot_general | solution.py:82
  128.9 3.3 %select_add_fusion.4 = f32[1024,768]{1,0:T(8,128)S(1)} fusion(f32[1024,768]{1,0:T(8,128)S(1)} %get-tuple-element.319, bf16[512,1024]{1,0:T(8,128)(2,1)} %get-tuple-element.286, pred[]{:T(512)S(6)} %compare.3, bf16[8,512,768]{2,1,0:T(8,128)(2,1)} %get-tuple-element.331, s32[]{:T(128)} %get-tuple-element.318), kind=kOutput, calls=%fused_computation.4.clone.1 | convolution fusion | flops 806879232 | bytes 8126977 | tf_op jit(solution)/shard_map/while/body/eval_jaxpr/dot_general | solution.py:88
  132.3 3.9 %convert_reduce_fusion.2 = (f32[1024]{0:T(1024)S(1)}, bf16[512,1024]{1,0:T(8,128)(2,1)}) fusion(f32[512]{0:T(512)S(1)} %bitcast.34, bf16[1024,768]{1,0:T(8,128)(2,1)} %get-tuple-element.332, bf16[8,512,768]{2,1,0:T(8,128)(2,1)} %get-tuple-element.331, s32[]{:T(128)} %get-tuple-element.318, f32[1024]{0:T(1024)S(1)} %get-tuple-element.330), kind=kOutput, calls=%fused_computation.5.clone.1 | convolution fusion | flops 808975360 | bytes 3418624 | tf_op jit(solution)/shard_map/while/body/eval_jaxpr/dot_general | solution.py:82
  136.2 3.3 %select_add_fusion.4 = f32[1024,768]{1,0:T(8,128)S(1)} fusion(f32[1024,768]{1,0:T(8,128)S(1)} %get-tuple-element.319, bf16[512,1024]{1,0:T(8,128)(2,1)} %get-tuple-element.286, pred[]{:T(512)S(6)} %compare.3, bf16[8,512,768]{2,1,0:T(8,128)(2,1)} %get-tuple-element.331, s32[]{:T(128)} %get-tuple-element.318), kind=kOutput, calls=%fused_computation.4.clone.1 | convolution fusion | flops 806879232 | bytes 8126977 | tf_op jit(solution)/shard_map/while/body/eval_jaxpr/dot_general | solution.py:88
  139.5 3.9 %convert_reduce_fusion.2 = (f32[1024]{0:T(1024)S(1)}, bf16[512,1024]{1,0:T(8,128)(2,1)}) fusion(f32[512]{0:T(512)S(1)} %bitcast.34, bf16[1024,768]{1,0:T(8,128)(2,1)} %get-tuple-element.332, bf16[8,512,768]{2,1,0:T(8,128)(2,1)} %get-tuple-element.331, s32[]{:T(128)} %get-tuple-element.318, f32[1024]{0:T(1024)S(1)} %get-tuple-element.330), kind=kOutput, calls=%fused_computation.5.clone.1 | convolution fusion | flops 808975360 | bytes 3418624 | tf_op jit(solution)/shard_map/while/body/eval_jaxpr/dot_general | solution.py:82
  143.4 3.3 %select_add_fusion.4 = f32[1024,768]{1,0:T(8,128)S(1)} fusion(f32[1024,768]{1,0:T(8,128)S(1)} %get-tuple-element.319, bf16[512,1024]{1,0:T(8,128)(2,1)} %get-tuple-element.286, pred[]{:T(512)S(6)} %compare.3, bf16[8,512,768]{2,1,0:T(8,128)(2,1)} %get-tuple-element.331, s32[]{:T(128)} %get-tuple-element.318), kind=kOutput, calls=%fused_computation.4.clone.1 | convolution fusion | flops 806879232 | bytes 8126977 | tf_op jit(solution)/shard_map/while/body/eval_jaxpr/dot_general | solution.py:88
  146.8 3.9 %convert_reduce_fusion.2 = (f32[1024]{0:T(1024)S(1)}, bf16[512,1024]{1,0:T(8,128)(2,1)}) fusion(f32[512]{0:T(512)S(1)} %bitcast.34, bf16[1024,768]{1,0:T(8,128)(2,1)} %get-tuple-element.332, bf16[8,512,768]{2,1,0:T(8,128)(2,1)} %get-tuple-element.331, s32[]{:T(128)} %get-tuple-element.318, f32[1024]{0:T(1024)S(1)} %get-tuple-element.330), kind=kOutput, calls=%fused_computation.5.clone.1 | convolution fusion | flops 808975360 | bytes 3418624 | tf_op jit(solution)/shard_map/while/body/eval_jaxpr/dot_general | solution.py:82
  150.7 3.3 %select_add_fusion.4 = f32[1024,768]{1,0:T(8,128)S(1)} fusion(f32[1024,768]{1,0:T(8,128)S(1)} %get-tuple-element.319, bf16[512,1024]{1,0:T(8,128)(2,1)} %get-tuple-element.286, pred[]{:T(512)S(6)} %compare.3, bf16[8,512,768]{2,1,0:T(8,128)(2,1)} %get-tuple-element.331, s32[]{:T(128)} %get-tuple-element.318), kind=kOutput, calls=%fused_computation.4.clone.1 | convolution fusion | flops 806879232 | bytes 8126977 | tf_op jit(solution)/shard_map/while/body/eval_jaxpr/dot_general | solution.py:88
  154.0 3.9 %convert_reduce_fusion.2 = (f32[1024]{0:T(1024)S(1)}, bf16[512,1024]{1,0:T(8,128)(2,1)}) fusion(f32[512]{0:T(512)S(1)} %bitcast.34, bf16[1024,768]{1,0:T(8,128)(2,1)} %get-tuple-element.332, bf16[8,512,768]{2,1,0:T(8,128)(2,1)} %get-tuple-element.331, s32[]{:T(128)} %get-tuple-element.318, f32[1024]{0:T(1024)S(1)} %get-tuple-element.330), kind=kOutput, calls=%fused_computation.5.clone.1 | convolution fusion | flops 808975360 | bytes 3418624 | tf_op jit(solution)/shard_map/while/body/eval_jaxpr/dot_general | solution.py:82
  157.9 3.3 %select_add_fusion.4 = f32[1024,768]{1,0:T(8,128)S(1)} fusion(f32[1024,768]{1,0:T(8,128)S(1)} %get-tuple-element.319, bf16[512,1024]{1,0:T(8,128)(2,1)} %get-tuple-element.286, pred[]{:T(512)S(6)} %compare.3, bf16[8,512,768]{2,1,0:T(8,128)(2,1)} %get-tuple-element.331, s32[]{:T(128)} %get-tuple-element.318), kind=kOutput, calls=%fused_computation.4.clone.1 | convolution fusion | flops 806879232 | bytes 8126977 | tf_op jit(solution)/shard_map/while/body/eval_jaxpr/dot_general | solution.py:88
  161.2 3.9 %convert_reduce_fusion.2 = (f32[1024]{0:T(1024)S(1)}, bf16[512,1024]{1,0:T(8,128)(2,1)}) fusion(f32[512]{0:T(512)S(1)} %bitcast.34, bf16[1024,768]{1,0:T(8,128)(2,1)} %get-tuple-element.332, bf16[8,512,768]{2,1,0:T(8,128)(2,1)} %get-tuple-element.331, s32[]{:T(128)} %get-tuple-element.318, f32[1024]{0:T(1024)S(1)} %get-tuple-element.330), kind=kOutput, calls=%fused_computation.5.clone.1 | convolution fusion | flops 808975360 | bytes 3418624 | tf_op jit(solution)/shard_map/while/body/eval_jaxpr/dot_general | solution.py:82
  165.1 3.3 %select_add_fusion.4 = f32[1024,768]{1,0:T(8,128)S(1)} fusion(f32[1024,768]{1,0:T(8,128)S(1)} %get-tuple-element.319, bf16[512,1024]{1,0:T(8,128)(2,1)} %get-tuple-element.286, pred[]{:T(512)S(6)} %compare.3, bf16[8,512,768]{2,1,0:T(8,128)(2,1)} %get-tuple-element.331, s32[]{:T(128)} %get-tuple-element.318), kind=kOutput, calls=%fused_computation.4.clone.1 | convolution fusion | flops 806879232 | bytes 8126977 | tf_op jit(solution)/shard_map/while/body/eval_jaxpr/dot_general | solution.py:88
  168.5 3.9 %convert_reduce_fusion.2 = (f32[1024]{0:T(1024)S(1)}, bf16[512,1024]{1,0:T(8,128)(2,1)}) fusion(f32[512]{0:T(512)S(1)} %bitcast.34, bf16[1024,768]{1,0:T(8,128)(2,1)} %get-tuple-element.332, bf16[8,512,768]{2,1,0:T(8,128)(2,1)} %get-tuple-element.331, s32[]{:T(128)} %get-tuple-element.318, f32[1024]{0:T(1024)S(1)} %get-tuple-element.330), kind=kOutput, calls=%fused_computation.5.clone.1 | convolution fusion | flops 808975360 | bytes 3418624 | tf_op jit(solution)/shard_map/while/body/eval_jaxpr/dot_general | solution.py:82
  172.4 3.3 %select_add_fusion.4 = f32[1024,768]{1,0:T(8,128)S(1)} fusion(f32[1024,768]{1,0:T(8,128)S(1)} %get-tuple-element.319, bf16[512,1024]{1,0:T(8,128)(2,1)} %get-tuple-element.286, pred[]{:T(512)S(6)} %compare.3, bf16[8,512,768]{2,1,0:T(8,128)(2,1)} %get-tuple-element.331, s32[]{:T(128)} %get-tuple-element.318), kind=kOutput, calls=%fused_computation.4.clone.1 | convolution fusion | flops 806879232 | bytes 8126977 | tf_op jit(solution)/shard_map/while/body/eval_jaxpr/dot_general | solution.py:88
  175.7 3.9 %convert_reduce_fusion.2 = (f32[1024]{0:T(1024)S(1)}, bf16[512,1024]{1,0:T(8,128)(2,1)}) fusion(f32[512]{0:T(512)S(1)} %bitcast.34, bf16[1024,768]{1,0:T(8,128)(2,1)} %get-tuple-element.332, bf16[8,512,768]{2,1,0:T(8,128)(2,1)} %get-tuple-element.331, s32[]{:T(128)} %get-tuple-element.318, f32[1024]{0:T(1024)S(1)} %get-tuple-element.330), kind=kOutput, calls=%fused_computation.5.clone.1 | convolution fusion | flops 808975360 | bytes 3418624 | tf_op jit(solution)/shard_map/while/body/eval_jaxpr/dot_general | solution.py:82
  185.4 50.3 %all_to_all.15 = f32[16,64,769]{2,1,0:T(8,128)} all-to-all(f32[16,64,769]{2,1,0:T(8,128)S(1)} %pad_maximum_fusion), channel_id=1, replica_groups=mesh['blk'=8,'rows'=16] {'rows'}, dimensions={0} | all-to-all | bytes 6299648 | tf_op jit(solution)/shard_map/all_to_all | solution.py:29
  238.9 33.1 %all-gather.2.cloned.1.call-done = f32[1024,769]{1,0:T(8,128)} async-done(((f32[64,769]{1,0:T(8,128)}), f32[1024,769]{1,0:T(8,128)}) %all-gather.2.cloned.1.call-update) | async-done | bytes 3149840 | tf_op jit(solution)/shard_map/all_gather | solution.py:50
  272.0 3.8 %split.18 = f32[1024,768]{1,0:T(8,128)} slice(f32[1024,769]{1,0:T(8,128)} %all-gather.2.cloned.1.call-done), slice={[0:1024], [0:768]} | slice | bytes 6291456 | tf_op jit(solution)/shard_map/split | solution.py:51
  (62 shorter events, 37.2 us)
Async XLA Ops:
  12.9 8.6 %copy-start = (bf16[1024,768]{1,0:T(8,128)(2,1)S(1)}, bf16[1024,768]{1,0:T(8,128)(2,1)}, u32[]{:S(2)}) copy-start(bf16[1024,768]{1,0:T(8,128)(2,1)} %param.8) | copy-start | bytes 4718596
  12.9 81.2 %all-to-all-start = ((bf16[8,512,768]{2,1,0:T(8,128)(2,1)}), bf16[8,512,768]{2,1,0:T(8,128)(2,1)}, u32[]{:S(2)}, u32[]{:S(2)}) async-start(bf16[8,512,768]{2,1,0:T(8,128)(2,1)} %stack.2), calls=%async_computation | async-start | bytes 12582912 | tf_op jit(solution)/shard_map/all_to_all | solution.py:75
  21.6 72.6 %copy-start.2 = (f32[1024]{0:T(1024)S(1)}, f32[1024]{0:T(1024)}, u32[]{:S(2)}) copy-start(f32[1024]{0:T(1024)} %param.9) | copy-start | bytes 12292
  113.4 4.5 %copy-start.1 = (bf16[1024,768]{1,0:T(8,128)(2,1)}, bf16[1024,768]{1,0:T(8,128)(2,1)S(1)}, u32[]{:S(2)}) copy-start(bf16[1024,768]{1,0:T(8,128)(2,1)S(1)} %get-tuple-element.340) | copy-start | bytes 4718596
  114.2 10.8 %all-to-all-start.1 = ((f32[8,8,512]{2,1,0:T(8,128)}), f32[8,8,512]{2,1,0:T(8,128)S(1)}, u32[]{:S(2)}, u32[]{:S(2)}) async-start(f32[8,8,512]{2,1,0:T(8,128)} %broadcast_in_dim.31), calls=%async_computation.1 | async-start | bytes 262144 | tf_op jit(solution)/shard_map/all_to_all | solution.py:13
  117.9 154.1 %all-gather.2.cloned.1.call-start = ((), (), s32[]{:S(2)}) async-start(), calls=%async_computation.3 | async-start | bytes 3899392 | tf_op jit(solution)/shard_map/all_gather | solution.py:50
Sparse Core Ops, SparseCore 0:
  239.0 32.9 all-gather.1
